TPU v7x, 256 devices: a whole 4x4x8 slice. The times are simulated.
256 devices in a mesh: fsdp: 16 (over z, core), cols: 16 (over y, x).
Axes of the slice: x: 4, y: 4, z: 8, core: 2. Of those that a mesh axis runs over, the one named last changes fastest.
Arguments:
- weight_gate: bfloat16 [4096, 11008], P('fsdp', 'cols'), may hold values from -0.09375 to 0.09375
- low_gate: bfloat16 [4096, 64], P('fsdp'), may hold values from -0.09375 to 0.09375
- high_gate: bfloat16 [64, 11008], P(None, 'cols'), may hold values from -0.75 to 0.75
- weight_up: bfloat16 [4096, 11008], P('fsdp', 'cols'), may hold values from -0.09375 to 0.09375
- low_up: bfloat16 [4096, 64], P('fsdp'), may hold values from -0.09375 to 0.09375
- high_up: bfloat16 [64, 11008], P(None, 'cols'), may hold values from -0.75 to 0.75
- weight_down: bfloat16 [11008, 4096], P('cols', 'fsdp'), may hold values from -0.0546875 to 0.0546875
- low_down: bfloat16 [11008, 64], P('cols'), may hold values from -0.0546875 to 0.0546875
- high_down: bfloat16 [64, 4096], P(None, 'fsdp'), may hold values from -0.75 to 0.75
- norm_train: float32 [4096], P(('fsdp', 'cols')), may hold values from 0.25 to 1.75
- norm_step: float32 [4096], P(('fsdp', 'cols')), may hold values from -0.3 to 0.3
Outputs:
- serve_gate: bfloat16 [11008, 4096], P('cols')
- serve_up: bfloat16 [11008, 4096], P('cols')
- serve_down: bfloat16 [4096, 11008], P(None, 'cols')
- serve_norm: bfloat16 [4096], replicated
All inputs are finite; a program needn't handle non-finite values.
Results may differ from a plain program's by a relative error of at most 0.001.
Values may be sent and summed in bfloat16 or wider, within the bound.
A program may use at most 128 MiB of HBM per device.

v0:
```python
import jax
import jax.numpy as jnp
from jax import lax
from jax.sharding import Mesh
from jax.sharding import PartitionSpec as P

FSDP = ("fsdp_0", "fsdp_1")
FSDP_COLS = ("fsdp_0", "fsdp_1", "cols_0", "cols_1")
COLS = ("cols_0", "cols_1")


mix_rate = 0.5


def gather_turned(arrays, axis, dims):
    turned = [jnp.moveaxis(a, dim, 0) for a, dim in zip(arrays, dims)]
    both = jnp.concatenate([t.reshape(len(t), -1) for t in turned], axis=1)
    out, at, finished = (lax.all_gather(both, axis, axis=0, tiled=True), 0, [])
    for t, dim in zip(turned, dims):
        section = out[:, at : at + t[0].size].reshape(-1, *t.shape[1:])
        finished.append(jnp.moveaxis(section, 0, dim))
        at += t[0].size
    return tuple(finished)


def joined_along(parts, dim):
    parts = jnp.moveaxis(parts, 0, dim)
    lengths = parts.shape
    return parts.reshape(*lengths[:dim], lengths[dim] * lengths[dim + 1], *lengths[dim + 2 :])


def gather_in_order(x, axes, turns):
    parts = x[None]
    for k in turns:
        parts = lax.all_gather(parts, axes[k], axis=0, tiled=True)
    current = [lax.axis_size(axes[k]) for k in reversed(turns)]
    parts = parts.reshape(*current, *x.shape)
    turned = sorted(range(len(turns)), key=lambda place: turns[len(turns) - 1 - place])
    return parts.transpose(*turned, *range(len(turns), parts.ndim)).reshape(-1, *x.shape)


def gather_axes(x, axes, turns, dim):
    return joined_along(gather_in_order(x, axes, turns), dim)


def per_device(
    weight_gate,
    low_gate,
    high_gate,
    weight_up,
    low_up,
    high_up,
    weight_down,
    low_down,
    high_down,
    norm_train,
    norm_step,
):
    fresh_gate = weight_gate.astype(jnp.float32) + mix_rate * jnp.dot(
        low_gate, high_gate, preferred_element_type=jnp.float32
    )
    fresh_up = weight_up.astype(jnp.float32) + mix_rate * jnp.dot(
        low_up, high_up, preferred_element_type=jnp.float32
    )
    fresh_down = weight_down.astype(jnp.float32) + mix_rate * jnp.dot(
        low_down, high_down, preferred_element_type=jnp.float32
    )
    narrow_gate, narrow_up, narrow_down = (
        fresh_gate.astype(jnp.bfloat16),
        fresh_up.astype(jnp.bfloat16),
        fresh_down.astype(jnp.bfloat16),
    )
    serve_gate, serve_up, serve_down = gather_turned(
        (narrow_gate, narrow_up, narrow_down), FSDP, (0, 0, 1)
    )
    serve_gate, serve_up, serve_down = (serve_gate.T, serve_up.T, serve_down.T)
    serve_norm = gather_axes(
        (norm_train + norm_step).astype(jnp.bfloat16), FSDP_COLS, (0, 2, 3, 1), 0
    )
    return (serve_gate, serve_up, serve_down, serve_norm)


def solution(mesh):
    finer = Mesh(mesh.devices.reshape(8, 2, 4, 4), ("fsdp_0", "fsdp_1", "cols_0", "cols_1"))
    in_specs = (
        P(FSDP, COLS),
        P(FSDP, None),
        P(None, COLS),
        P(FSDP, COLS),
        P(FSDP, None),
        P(None, COLS),
        P(COLS, FSDP),
        P(COLS, None),
        P(None, FSDP),
        P(FSDP_COLS),
        P(FSDP_COLS),
    )
    out_specs = (P(COLS, None), P(COLS, None), P(None, COLS), P())
    return jax.shard_map(
        per_device, mesh=finer, in_specs=in_specs, out_specs=out_specs, check_vma=False
    )
```

profile of v0, /device:TPU:1, one launch (start us, length us, event | category | flops | bytes accessed | tf_op | source)
XLA Modules:
  0.0 139.9 jit_solution(2399572348826696943)
XLA Ops:
  7.2 0.0 copy-start
  7.2 0.0 all-gather.4.cloned.1.call-start
  7.2 0.8 copy-done
  8.1 1.3 fusion.3
  9.4 1.4 fusion.4
  10.7 0.0 copy-start.3
  10.8 0.0 copy-start.1
  10.8 0.0 copy-start.2
  10.8 1.3 fusion.6
  12.1 1.0 pad_maximum_fusion
  13.2 0.0 all-gather.4.cloned.1.call-update
  13.2 0.0 copy-done.3
  13.2 0.6 dynamic-slice
  14.4 0.0 copy-done.1
  14.4 0.0 copy-done.2
  14.5 0.2 dynamic-update-slice
  14.7 17.3 %all-reduce = bf16[128]{0:T(256)(128)(2,1)S(1)} all-reduce(bf16[128]{0:T(256)(128)(2,1)S(1)} %dynamic-update-slice), channel_id=2, replica_groups=mesh['fsdp_0'=8,'fsdp_1'=2,'cols_0'=4,'cols_1'=4] {'fsdp_0'}, use_global_device_ids=true, to_apply=%add | all-reduce | flops 128 | bytes 512
  32.0 0.1 reshape.12
  32.1 9.7 %all_gather.17 = bf16[32,16]{1,0:T(8,128)(2,1)S(1)} all-gather(bf16[8,16]{1,0:T(8,128)(2,1)S(1)} %reshape.12), channel_id=1, replica_groups=mesh['fsdp_0'=8,'fsdp_1'=2,'cols_0'=4,'cols_1'=4] {'cols_0'}, dimensions={0}, use_global_device_ids=true | all-gather | bytes 1280 | tf_op jit(solution)/shard_map/all_gather | solution.py:35
  41.8 0.1 copy.16
  41.9 10.1 %all-gather.1 = bf16[4,32,16]{1,2,0:T(8,128)(2,1)S(1)} all-gather(bf16[1,32,16]{1,2,0:T(8,128)(2,1)S(1)} %copy.16), channel_id=1, replica_groups=mesh['fsdp_0'=8,'fsdp_1'=2,'cols_0'=4,'cols_1'=4] {'cols_1'}, dimensions={0}, use_global_device_ids=true | all-gather | bytes 5120 | tf_op jit(solution)/shard_map/all_gather | solution.py:35
  52.0 0.1 copy.17
  52.1 10.0 %all_gather.19 = bf16[256,16]{1,0:T(8,128)(2,1)S(1)} all-gather(bf16[128,16]{1,0:T(8,128)(2,1)S(1)} %bitcast.19), channel_id=1, replica_groups=mesh['fsdp_0'=8,'fsdp_1'=2,'cols_0'=4,'cols_1'=4] {'fsdp_1'}, dimensions={0}, use_global_device_ids=true | all-gather | bytes 12288 | tf_op jit(solution)/shard_map/all_gather | solution.py:35
  62.1 0.7 reshape_reshape.3
  62.8 57.0 %all-gather.4.cloned.1.call-done = bf16[4096,2064]{0,1:T(8,128)(2,1)} async-done(((bf16[256,2064]{0,1:T(8,128)(2,1)}), bf16[4096,2064]{0,1:T(8,128)(2,1)}) %all-gather.4.cloned.1.call-update) | async-done | bytes 16908304 | tf_op jit(solution)/shard_map/all_gather | solution.py:18
  119.8 13.3 %fusion.7 = (bf16[4096,688]{0,1:T(8,128)(2,1)}, bf16[688,4096]{1,0:T(8,128)(2,1)}, bf16[688,4096]{1,0:T(8,128)(2,1)}) fusion(bf16[4096,2064]{0,1:T(8,128)(2,1)} %all-gather.4.cloned.1.call-done), kind=kLoop, calls=%fused_computation.14 | loop fusion | bytes 33816576 | tf_op jit(solution)/shard_map/slice | solution.py:20
  (3 shorter events, 0.0 us)
Async XLA Ops:
  7.2 0.9 copy-start
  7.2 112.6 %all-gather.4.cloned.1.call-start = ((), (), s32[]{:S(2)}) async-start(), calls=%async_computation | async-start | bytes 17965056 | tf_op jit(solution)/shard_map/all_gather | solution.py:18
  10.7 2.5 %copy-start.3 = (u32[256]{0:T(256)S(1)}, u32[256]{0:T(256)}, u32[]{:S(2)}) copy-start(u32[256]{0:T(256)} %constant.7) | copy-start | bytes 3076
  10.8 3.7 %copy-start.1 = (f32[16]{0:T(128)S(1)}, f32[16]{0:T(128)}, u32[]{:S(2)}) copy-start(f32[16]{0:T(128)} %param.20) | copy-start | bytes 196
  10.8 3.7 %copy-start.2 = (f32[16]{0:T(128)S(1)}, f32[16]{0:T(128)}, u32[]{:S(2)}) copy-start(f32[16]{0:T(128)} %param.21) | copy-start | bytes 196
Sparse Core Ops, SparseCore 0:
  13.3 106.4 all-gather.3
where the time goes:
time: 140 us
  waiting for transfers between devices  57 us (41%)
  blocking collectives  47.1 us (34%)
  local copies, waits for them, and re-layouts  16 us (11%)
  between operations  14.8 us (11%)
  matrix products  4 us (3%)
    all_gather x1, waiting for transfers between devices, gather_turned(): out, at, finished = (lax.all_gather(both, axis, axis=0, tiled=True), 0, [])  57 us
    all_gather x3, blocking collectives, gather_in_order(): parts = lax.all_gather(parts, axes[k], axis=0, tiled=True)  29.8 us
    unnamed x1, blocking collectives  17.3 us
    slice x1, local copies, waits for them, and re-layouts, gather_turned(): section = out[:, at:at + t[0].size].reshape(-1, *t.shape[1:])  13.3 us
  transfers between devices with their start and end apart: 1, of which 1 were waited for; matrix products, arithmetic and copies ran while one was open for 1% of the time, Pallas kernels for 0%

commit v1 on v0

v1 whole, which is shorter than its diff:
```python
import jax
import jax.numpy as jnp
from jax import lax
from jax.experimental import pallas as pl
from jax.experimental.pallas import tpu as pltpu
from jax.sharding import PartitionSpec as P

mix_rate = 0.5
MESH = pl.DeviceIdType.MESH
DMA = pltpu.SemaphoreType.DMA


def kernel(nf, nc, cut, *refs):
    ins, outs, norm_out = refs[0:11], refs[11:14], refs[14]
    held, norm_all = refs[15:26], refs[26]
    (in_sem, ring_send, ring_recv, pair_send, pair_recv, n1_send, n1_recv, n2_send, n2_recv) = refs[27:]
    nz = nf // 2
    far, near = nz // 2, nz // 2 - 1
    rows, width = ins[0].shape
    f, c = lax.axis_index("fsdp"), lax.axis_index("cols")
    z, core = f // 2, f % 2
    partner = z * 2 + 1 - core

    def at(dz):
        return lax.rem(z + dz + nz, nz) * 2 + core

    barrier = pltpu.get_barrier_semaphore()
    for k in range(1, nf):
        pl.semaphore_signal(barrier, inc=1, device_id={"fsdp": lax.rem(f + k, nf)}, device_id_type=MESH)
    for k in range(1, nc):
        pl.semaphore_signal(barrier, inc=1, device_id={"cols": lax.rem(c + k, nc)}, device_id_type=MESH)

    loads = [pltpu.make_async_copy(ins[i], held[i], in_sem.at[i]) for i in range(11)]
    for load in loads:
        load.start()

    def columns(source):
        return pl.ds(pl.multiple_of(source * width, width), width)

    def merge(a):
        for i in range(3 * a, 3 * a + 3):
            loads[i].wait()
        w, left, right = held[3 * a], held[3 * a + 1], held[3 * a + 2]
        product = lax.dot_general(
            left[...], right[...], (((0,), (0,)), ((), ())), preferred_element_type=jnp.float32
        )
        fresh = w[...].astype(jnp.float32) + mix_rate * product
        outs[a][:, columns(f)] = fresh.astype(jnp.bfloat16)

    spans = [[(0, cut), (cut, rows - cut)] for _ in range(3)]

    def block(a, half, source):
        start, size = spans[a][half]
        return outs[a].at[pl.ds(start, size), columns(source)]

    def hops(way, half):
        return far if way == half else near

    order = [[(a, half) for half in (way, 1 - way) for a in range(3)] for way in (0, 1)]

    def ring(way, step, a, half):
        source = at(-(step - 1) if way == 0 else step - 1)
        piece = block(a, half, source)
        return pltpu.make_async_remote_copy(
            src_ref=piece,
            dst_ref=piece,
            send_sem=ring_send.at[way, a, half],
            recv_sem=ring_recv.at[way, step - 1, a, half],
            device_id={"fsdp": at(1 if way == 0 else -1)},
            device_id_type=MESH,
        )

    def arrival(way, step, a, half):
        source = at(-step if way == 0 else step)
        piece = block(a, half, source)
        return pltpu.make_async_remote_copy(
            src_ref=piece,
            dst_ref=piece,
            send_sem=ring_send.at[way, a, half],
            recv_sem=ring_recv.at[way, step - 1, a, half],
            device_id={"fsdp": at(1 if way == 0 else -1)},
            device_id_type=MESH,
        )

    def to_partner(ref, a):
        return pltpu.make_async_remote_copy(
            src_ref=ref,
            dst_ref=ref,
            send_sem=pair_send.at[a],
            recv_sem=pair_recv.at[a],
            device_id={"fsdp": partner},
            device_id_type=MESH,
        )

    def send_own(a):
        for half in (0, 1):
            for way in (0, 1):
                ring(way, 1, a, half if way == 0 else 1 - half).start()
        to_partner(outs[a].at[:, columns(f)], a).start()

    loads[9].wait()
    loads[10].wait()
    gain = (held[9][...] + held[10][...]).astype(jnp.bfloat16)
    short = gain.shape[1]
    lanes = short * nc
    place = lax.broadcasted_iota(jnp.int32, (short, lanes), 1) == (
        lax.broadcasted_iota(jnp.int32, (short, lanes), 0) + c * short
    )
    placed = jnp.dot(
        jnp.broadcast_to(gain, (16, short)),
        place.astype(jnp.bfloat16),
        preferred_element_type=jnp.float32,
    )
    norm_all[c, f] = placed[0:1]

    merge(0)
    merge(1)
    pl.semaphore_wait(barrier, nf + nc - 2)

    def n1(k):
        row = norm_all.at[c, f]
        return pltpu.make_async_remote_copy(
            src_ref=row,
            dst_ref=row,
            send_sem=n1_send,
            recv_sem=n1_recv,
            device_id={"fsdp": lax.rem(f + k, nf)},
            device_id_type=MESH,
        )

    def n2(k):
        part = norm_all.at[c]
        return pltpu.make_async_remote_copy(
            src_ref=part,
            dst_ref=part,
            send_sem=n2_send,
            recv_sem=n2_recv,
            device_id={"cols": lax.rem(c + k, nc)},
            device_id_type=MESH,
        )

    for k in range(1, nf):
        n1(k).start()
    send_own(0)
    merge(2)
    send_own(1)
    send_own(2)

    def take(step):
        for i in range(6):
            for way in (0, 1):
                a, half = order[way][i]
                if step <= hops(way, half):
                    arrival(way, step, a, half).wait_recv()
                    if step < hops(way, half):
                        ring(way, step + 1, a, half).start()
                    source = at(-step if way == 0 else step)
                    to_partner(block(a, half, source), a).start()

    def wait_bytes(ref, sem):
        pltpu.make_async_copy(ref, ref, sem).wait()

    for step in range(1, far + 1):
        take(step)
        if step == 1:
            wait_bytes(norm_all.at[0, pl.ds(0, nf - 1)], n1_recv)
            for k in range(1, nc):
                n2(k).start()

    if nc > 1:
        wait_bytes(norm_all.at[pl.ds(0, nc - 1)], n2_recv)
        wait_bytes(norm_all.at[pl.ds(0, nc - 1)], n2_send)
    wait_bytes(norm_all.at[0, pl.ds(0, nf - 1)], n1_send)
    total = norm_all[0]
    for k in range(1, nc):
        total = total + norm_all[k]
    norm_out[...] = total

    for way in (0, 1):
        for a in range(3):
            for half in (0, 1):
                start, size = spans[a][half]
                wait_bytes(
                    outs[a].at[pl.ds(start, size), pl.ds(0, hops(way, half) * width)],
                    ring_send.at[way, a, half],
                )
    for a in range(3):
        wait_bytes(outs[a].at[:, pl.ds(0, nz * width)], pair_send.at[a])
        wait_bytes(outs[a].at[:, pl.ds(0, nz * width)], pair_recv.at[a])


def solution(mesh):
    nf, nc = mesh.shape["fsdp"], mesh.shape["cols"]

    def per_device(
        weight_gate, low_gate, high_gate, weight_up, low_up, high_up,
        weight_down, low_down, high_down, norm_train, norm_step,
    ):
        rows, width = weight_down.shape
        rank = low_down.shape[1]
        short = norm_train.shape[0]
        cut = (rows // 2 + 15) // 16 * 16
        far = nf // 4
        big = jax.ShapeDtypeStruct((rows, width * nf), jnp.bfloat16)
        gate, up, down, norm = pl.pallas_call(
            lambda *refs: kernel(nf, nc, cut, *refs),
            out_shape=(big, big, big, jax.ShapeDtypeStruct((nf, 1, short * nc), jnp.float32)),
            in_specs=[pl.BlockSpec(memory_space=pltpu.HBM)] * 11,
            out_specs=(pl.BlockSpec(memory_space=pltpu.VMEM),) * 4,
            scratch_shapes=[
                pltpu.VMEM((rows, width), jnp.bfloat16),
                pltpu.VMEM((rank, rows), jnp.bfloat16),
                pltpu.VMEM((rank, width), jnp.bfloat16),
            ] * 3
            + [
                pltpu.VMEM((1, short), jnp.float32),
                pltpu.VMEM((1, short), jnp.float32),
                pltpu.VMEM((nc, nf, 1, short * nc), jnp.float32),
                DMA((11,)),
                DMA((2, 3, 2)),
                DMA((2, far, 3, 2)),
                DMA((3,)),
                DMA((3,)),
                DMA, DMA, DMA, DMA,
            ],
            compiler_params=pltpu.CompilerParams(
                collective_id=0, has_side_effects=True, vmem_limit_bytes=VMEM_LIMIT
            ),
        )(*[pltpu.with_memory_space_constraint(x, pltpu.HBM) for x in (
            weight_gate.T, high_gate, low_gate.T,
            weight_up.T, high_up, low_up.T,
            weight_down, low_down.T, high_down,
            norm_train.reshape(1, short), norm_step.reshape(1, short),
        )])
        return gate, up, down.T, norm.astype(jnp.bfloat16).reshape(-1)

    both = ("fsdp", "cols")
    return jax.shard_map(
        per_device,
        mesh=mesh,
        in_specs=(
            P("fsdp", "cols"), P("fsdp", None), P(None, "cols"),
            P("fsdp", "cols"), P("fsdp", None), P(None, "cols"),
            P("cols", "fsdp"), P("cols", None), P(None, "fsdp"),
            P(both), P(both),
        ),
        out_specs=(P("cols", None), P("cols", None), P(None, "cols"), P()),
        check_vma=False,
    )


VMEM_LIMIT = 24 * 1024 * 1024
```

time: 140 us -> 104 us (0.74)
  Pallas kernels: 0 us -> 95.5 us
  waiting for transfers between devices: 57 us -> 0 us
  blocking collectives: 47.1 us -> 0 us
  between operations: 14.8 us -> 0.65 us
  local copies, waits for them, and re-layouts: 16 us -> 8.07 us
  matrix products: 4 us -> 0 us
    pallas_call x0 -> x1, Pallas kernels: none -> 95.5 us  [per_device(): pl.pallas_call(lambda *refs: kernel(nf, nc, cut, *refs), out_shape=(big,...]
    all_gather x1 -> x0, waiting for transfers between devices: 57 us -> none  [gather_turned(): out, at, finished = (lax.all_gather(both, axis, axis=0, tiled=True), 0, [])]
    all_gather x3 -> x0, blocking collectives: 29.8 us -> none  [gather_in_order(): parts = lax.all_gather(parts, axes[k], axis=0, tiled=True)]
    unnamed x1 -> x0, blocking collectives: 17.3 us -> none
    slice x1 -> x0, local copies, waits for them, and re-layouts: 13.3 us -> none  [gather_turned(): section = out[:, at:at + t[0].size].reshape(-1, *t.shape[1:])]
    unnamed x12 -> x4, local copies, waits for them, and re-layouts: 1.78 us -> 8.07 us
    dot_general x3 -> x0, matrix products: 4 us -> none  [the longest x1 1.36 us: per_device(): jnp.dot(low_up, high_up, preferred_element_type=jnp.float32)]
  transfers between devices with their start and end apart: 1 -> 0, of which waited for: 1 -> 0; matrix products, arithmetic and copies ran while one was open for 1% -> 0% of each run, Pallas kernels for 0% -> 0%
where the time goes in v1:
time: 104 us
  Pallas kernels  95.5 us (92%)
  local copies, waits for them, and re-layouts  8.07 us (8%)
    pallas_call x1, Pallas kernels, per_device(): pl.pallas_call(lambda *refs: kernel(nf, nc, cut, *refs), out_shape=(big,...  95.5 us
    unnamed x4, local copies, waits for them, and re-layouts  8.07 us

profile of v1, /device:TPU:1, one launch (start us, length us, event | category | flops | bytes accessed | tf_op | source)
XLA Modules:
  0.0 104.3 jit_solution(9871449388055224855)
XLA Ops:
  0.6 95.5 %shard_map.138 = (bf16[688,4096]{1,0:T(8,128)(2,1)S(1)}, bf16[688,4096]{1,0:T(8,128)(2,1)S(1)}, bf16[688,4096]{1,0:T(8,128)(2,1)S(1)}, f32[16,1,256]{2,1,0:T(1,128)S(1)}) custom-call(bf16[688,256]{1,0:T(8,128)(2,1)} %bitcast.11, bf16[64,688]{1,0:T(8,128)(2,1)} %refs_1_.1, bf16[64,256]{1,0:T(8,128)(2,1)} %bitcast.14, bf16[688,256]{1,0:T(8,128)(2,1)} %bitcast.12, ...), custom_call_target="tpu_custom_call" | custom-call | tf_op jit(solution)/shard_map/pallas_call | solution.py:205
  96.2 0.1 convert_reduce_fusion
  96.2 0.6 copy.15
  96.8 2.5 %copy.19 = bf16[688,4096]{1,0:T(8,128)(2,1)} copy(bf16[688,4096]{1,0:T(8,128)(2,1)S(1)} %get-tuple-element.16) | data formatting | bytes 11272192
  99.3 2.5 %copy.20 = bf16[688,4096]{1,0:T(8,128)(2,1)} copy(bf16[688,4096]{1,0:T(8,128)(2,1)S(1)} %get-tuple-element.17) | data formatting | bytes 11272192
  101.8 2.5 %copy.21 = bf16[4096,688]{0,1:T(8,128)(2,1)} copy(bf16[4096,688]{0,1:T(8,128)(2,1)S(1)} %bitcast.10) | data formatting | bytes 11272192

commit v2 on v1

v2 whole, which is shorter than its diff:
```python
import jax
import jax.numpy as jnp
from jax import lax
from jax.experimental import pallas as pl
from jax.experimental.pallas import tpu as pltpu
from jax.sharding import PartitionSpec as P

mix_rate = 0.5
MESH = pl.DeviceIdType.MESH
DMA = pltpu.SemaphoreType.DMA
LANES = 128
VMEM_LIMIT = 24 * 1024 * 1024


def gather_kernel(nf, nx, ny, cut, *refs):
    ins, outs, norm_rows = refs[0:11], refs[11:14], refs[14]
    held, norm_plane = refs[15:26], refs[26]
    (
        in_sem, ring_send, ring_recv, pair_send, pair_recv,
        x_send, x_recv, y_send, y_recv, n_send, n_recv, np_send, np_recv,
    ) = refs[27:]
    nz = nf // 2
    far, near = nz // 2, nz // 2 - 1
    rows, width = ins[0].shape
    f, c = lax.axis_index("fsdp"), lax.axis_index("cols")
    z, core = f // 2, f % 2
    y, x = c // nx, c % nx
    partner = z * 2 + 1 - core

    def at_z(dz):
        return lax.rem(z + dz + nz, nz) * 2 + core

    def at_x(dx):
        return y * nx + lax.rem(x + dx + nx, nx)

    def at_y(dy):
        return lax.rem(y + dy + ny, ny) * nx + x

    near_by = [("fsdp", partner)]
    near_by += [("fsdp", at_z(d)) for d in ((1, -1) if nz > 2 else (1,) if nz > 1 else ())]
    near_by += [("cols", at_x(d)) for d in ((1, -1) if nx > 2 else (1,) if nx > 1 else ())]
    near_by += [("cols", at_y(d)) for d in ((1, -1) if ny > 2 else (1,) if ny > 1 else ())]
    barrier = pltpu.get_barrier_semaphore()
    for axis, index in near_by:
        pl.semaphore_signal(barrier, inc=1, device_id={axis: index}, device_id_type=MESH)

    loads = [pltpu.make_async_copy(ins[i], held[i], in_sem.at[i]) for i in range(11)]
    for load in loads:
        load.start()

    def send(ref, axis, index, send_sem, recv_sem):
        return pltpu.make_async_remote_copy(
            src_ref=ref,
            dst_ref=ref,
            send_sem=send_sem,
            recv_sem=recv_sem,
            device_id={axis: index},
            device_id_type=MESH,
        )

    def wait_bytes(ref, sem):
        pltpu.make_async_copy(ref, ref, sem).wait()

    def columns(source):
        return pl.ds(pl.multiple_of(source * width, width), width)

    spans = [(0, cut), (cut, rows - cut)]

    def merge(a):
        for i in range(3 * a, 3 * a + 3):
            loads[i].wait()
        w, left, right = held[3 * a], held[3 * a + 1], held[3 * a + 2]
        product = lax.dot_general(
            left[...], right[...], (((0,), (0,)), ((), ())), preferred_element_type=jnp.float32
        )
        fresh = w[...].astype(jnp.float32) + mix_rate * product
        outs[a][:, columns(f)] = fresh.astype(jnp.bfloat16)

    def block(a, half, source):
        start, size = spans[half]
        return outs[a].at[pl.ds(start, size), columns(source)]

    def hops(way, half):
        return far if way == half else near

    order = [[(a, half) for half in (way, 1 - way) for a in range(3)] for way in (0, 1)]
    ahead = (1, -1)

    def ring(way, step, a, half):
        return send(
            block(a, half, at_z(-ahead[way] * (step - 1))),
            "fsdp",
            at_z(ahead[way]),
            ring_send.at[way, a, half],
            ring_recv.at[way, step - 1, a, half],
        )

    def to_partner(ref, a):
        return send(ref, "fsdp", partner, pair_send.at[a], pair_recv.at[a])

    def norm_hops(way):
        return hops(way, 0)

    def norm_ring(way, step):
        return send(
            norm_rows.at[at_z(-ahead[way] * (step - 1))],
            "fsdp",
            at_z(ahead[way]),
            n_send.at[way, step - 1],
            n_recv.at[way, step - 1],
        )

    def norm_to_partner(source):
        return send(norm_rows.at[source], "fsdp", partner, np_send, np_recv)

    loads[9].wait()
    loads[10].wait()
    gain = (held[9][...] + held[10][...]).astype(jnp.bfloat16)
    short = gain.shape[1]
    tiles = norm_rows.shape[1]
    spread = lax.broadcasted_iota(jnp.int32, (short, LANES), 1)
    index = lax.broadcasted_iota(jnp.int32, (short, LANES), 0) + c * short
    for t in range(tiles):
        place = (spread + t * LANES == index).astype(jnp.bfloat16)
        placed = jnp.dot(
            jnp.broadcast_to(gain, (16, short)), place, preferred_element_type=jnp.float32
        )
        norm_plane[y, x, t : t + 1] = placed[0:1]

    merge(0)
    merge(1)
    pl.semaphore_wait(barrier, len(near_by))

    def send_own(i):
        for way in (0, 1):
            a, half = order[way][i]
            ring(way, 1, a, half).start()

    def x_hop(way, step):
        source = lax.rem(x - ahead[way] * (step - 1) + nx, nx)
        return send(
            norm_plane.at[y, source], "cols", at_x(ahead[way]),
            x_send.at[way, step - 1], x_recv.at[way, step - 1],
        )

    def y_hop(way, step):
        source = lax.rem(y - ahead[way] * (step - 1) + ny, ny)
        return send(
            norm_plane.at[source], "cols", at_y(ahead[way]),
            y_send.at[way, step - 1], y_recv.at[way, step - 1],
        )

    def around(hop, n):
        counts = (n // 2, n - 1 - n // 2)
        for way in (0, 1):
            if counts[way] > 0:
                hop(way, 1).start()
        yield
        for step in range(1, max(counts) + 1):
            for way in (0, 1):
                if step <= counts[way]:
                    hop(way, step).wait_recv()
                    if step < counts[way]:
                        hop(way, step + 1).start()
        for way in (0, 1):
            for step in range(1, counts[way] + 1):
                hop(way, step).wait_send()

    xs, ys = around(x_hop, nx), around(y_hop, ny)
    next(xs)
    send_own(0)
    send_own(1)
    merge(2)
    send_own(2)
    for _ in xs:
        pass
    next(ys)
    to_partner(outs[0].at[:, columns(f)], 0).start()
    to_partner(outs[1].at[:, columns(f)], 1).start()
    for _ in ys:
        pass
    total = jnp.zeros((tiles, LANES), jnp.float32)
    for j in range(ny):
        for i in range(nx):
            total = total + norm_plane[j, i]
    norm_rows[f] = total
    to_partner(outs[2].at[:, columns(f)], 2).start()
    send_own(3)
    for way in (0, 1):
        if norm_hops(way) > 0:
            norm_ring(way, 1).start()
    norm_to_partner(f).start()
    send_own(4)
    send_own(5)

    for step in range(1, far + 1):
        for i in range(6):
            for way in (0, 1):
                a, half = order[way][i]
                if step <= hops(way, half):
                    ring(way, step, a, half).wait_recv()
                    if step < hops(way, half):
                        ring(way, step + 1, a, half).start()
                    to_partner(block(a, half, at_z(-ahead[way] * step)), a).start()
            if i == 2:
                for way in (0, 1):
                    if step <= norm_hops(way):
                        norm_ring(way, step).wait_recv()
                        if step < norm_hops(way):
                            norm_ring(way, step + 1).start()
                        norm_to_partner(at_z(-ahead[way] * step)).start()

    for way in (0, 1):
        for step in range(1, norm_hops(way) + 1):
            norm_ring(way, step).wait_send()
        for a in range(3):
            for half in (0, 1):
                start, size = spans[half]
                if hops(way, half) > 0:
                    wait_bytes(
                        outs[a].at[pl.ds(start, size), pl.ds(0, hops(way, half) * width)],
                        ring_send.at[way, a, half],
                    )
    wait_bytes(norm_rows.at[pl.ds(0, nz)], np_send)
    wait_bytes(norm_rows.at[pl.ds(0, nz)], np_recv)
    for a in range(3):
        wait_bytes(outs[a].at[:, pl.ds(0, nz * width)], pair_send.at[a])
        wait_bytes(outs[a].at[:, pl.ds(0, nz * width)], pair_recv.at[a])


def store_kernel(parts, *refs):
    ins, norm_rows, outs, norm_out = refs[0:3], refs[3], refs[4:7], refs[7]
    wide, narrow, sems, norm_sem = refs[8:]
    rows = ins[0].shape[0]
    size = -(-rows // (16 * parts)) * 16
    copies = []
    for a in range(3):
        for k in range(-(-rows // size)):
            span = pl.ds(k * size, min(size, rows - k * size))
            copies.append(
                pltpu.make_async_copy(ins[a].at[span], outs[a].at[span], sems.at[a, k])
            )
    for copy in copies:
        copy.start()
    count, tiles = norm_rows.shape[0:2]
    for i in range(count):
        wide[i * tiles : (i + 1) * tiles] = norm_rows[i]
    narrow[...] = wide[...].astype(jnp.bfloat16)
    last = pltpu.make_async_copy(narrow, norm_out, norm_sem)
    last.start()
    for copy in copies:
        copy.wait()
    last.wait()


def solution(mesh):
    nf, nc = mesh.shape["fsdp"], mesh.shape["cols"]
    nx = 4 if nc == 16 else 2 if nc == 4 else nc
    ny = nc // nx
    vmem, hbm = pl.BlockSpec(memory_space=pltpu.VMEM), pl.BlockSpec(memory_space=pltpu.HBM)

    def per_device(
        weight_gate, low_gate, high_gate, weight_up, low_up, high_up,
        weight_down, low_down, high_down, norm_train, norm_step,
    ):
        rows, width = weight_down.shape
        rank = low_down.shape[1]
        short = norm_train.shape[0]
        tiles = short * nc // LANES
        cut = (rows // 2 + 15) // 16 * 16
        far = nf // 4
        big = jax.ShapeDtypeStruct((rows, width * nf), jnp.bfloat16)
        whole = pl.pallas_call(
            lambda *refs: gather_kernel(nf, nx, ny, cut, *refs),
            out_shape=(big, big, big, jax.ShapeDtypeStruct((nf, tiles, LANES), jnp.float32)),
            in_specs=[hbm] * 11,
            out_specs=(vmem,) * 4,
            scratch_shapes=[
                pltpu.VMEM((rows, width), jnp.bfloat16),
                pltpu.VMEM((rank, rows), jnp.bfloat16),
                pltpu.VMEM((rank, width), jnp.bfloat16),
            ] * 3
            + [
                pltpu.VMEM((1, short), jnp.float32),
                pltpu.VMEM((1, short), jnp.float32),
                pltpu.VMEM((ny, nx, tiles, LANES), jnp.float32),
                DMA((11,)),
                DMA((2, 3, 2)),
                DMA((2, far, 3, 2)),
                DMA((3,)),
                DMA((3,)),
                DMA((2, 2)), DMA((2, 2)), DMA((2, 2)), DMA((2, 2)),
                DMA((2, far)), DMA((2, far)), DMA, DMA,
            ],
            compiler_params=pltpu.CompilerParams(
                collective_id=0, has_side_effects=True, vmem_limit_bytes=VMEM_LIMIT
            ),
        )(*[pltpu.with_memory_space_constraint(operand, pltpu.HBM) for operand in (
            weight_gate.T, high_gate, low_gate.T,
            weight_up.T, high_up, low_up.T,
            weight_down, low_down.T, high_down,
            norm_train.reshape(1, short), norm_step.reshape(1, short),
        )])
        parts = 4
        gate, up, down, norm = pl.pallas_call(
            lambda *refs: store_kernel(parts, *refs),
            out_shape=(big, big, big, jax.ShapeDtypeStruct((nf * tiles, LANES), jnp.bfloat16)),
            in_specs=[vmem] * 4,
            out_specs=(hbm,) * 4,
            scratch_shapes=[
                pltpu.VMEM((nf * tiles, LANES), jnp.float32),
                pltpu.VMEM((nf * tiles, LANES), jnp.bfloat16),
                DMA((3, parts)),
                DMA,
            ],
            compiler_params=pltpu.CompilerParams(vmem_limit_bytes=VMEM_LIMIT),
        )(*whole)
        return gate, up, down.T, norm.reshape(-1)

    both = ("fsdp", "cols")
    return jax.shard_map(
        per_device,
        mesh=mesh,
        in_specs=(
            P("fsdp", "cols"), P("fsdp", None), P(None, "cols"),
            P("fsdp", "cols"), P("fsdp", None), P(None, "cols"),
            P("cols", "fsdp"), P("cols", None), P(None, "fsdp"),
            P(both), P(both),
        ),
        out_specs=(P("cols", None), P("cols", None), P(None, "cols"), P()),
        check_vma=False,
    )
```

time: 104 us -> 99.5 us (0.957)
  local copies, waits for them, and re-layouts: 8.07 us -> 0 us
  Pallas kernels: 95.5 us -> 98.7 us
    unnamed x4 -> x0, local copies, waits for them, and re-layouts: 8.07 us -> none
    pallas_call x1 -> x2, Pallas kernels: 95.5 us -> 98.7 us  [the longest x1 92.7 us: per_device(): pl.pallas_call(lambda *refs: gather_kernel(nf, nx, ny, cut, *refs), out_s...]
where the time goes in v2:
time: 99.5 us; the launch traced here: 99.4 us
  Pallas kernels  98.7 us (99%)
    pallas_call x1, Pallas kernels, per_device(): pl.pallas_call(lambda *refs: gather_kernel(nf, nx, ny, cut, *refs), out_s...  92.7 us
    pallas_call x1, Pallas kernels, per_device(): pl.pallas_call(lambda *refs: store_kernel(parts, *refs), out_shape=(big,...  5.99 us

profile of v2, /device:TPU:1, one launch (start us, length us, event | category | flops | bytes accessed | tf_op | source)
XLA Modules:
  0.0 99.4 jit_solution(15571296252936490560)
XLA Ops:
  0.6 92.7 %shard_map.138 = (bf16[688,4096]{1,0:T(8,128)(2,1)S(1)}, bf16[688,4096]{1,0:T(8,128)(2,1)S(1)}, bf16[688,4096]{1,0:T(8,128)(2,1)S(1)}, f32[16,2,128]{2,1,0:T(2,128)S(1)}) custom-call(bf16[688,256]{1,0:T(8,128)(2,1)} %bitcast.9, bf16[64,688]{1,0:T(8,128)(2,1)} %refs_1_.1, bf16[64,256]{1,0:T(8,128)(2,1)} %bitcast.12, bf16[688,256]{1,0:T(8,128)(2,1)} %bitcast.10, ...), custom_call_target="tpu_custom_call" | custom-call | tf_op jit(solution)/shard_map/pallas_call | solution.py:273
  93.4 6.0 %shard_map.139 = (bf16[688,4096]{1,0:T(8,128)(2,1)}, bf16[688,4096]{1,0:T(8,128)(2,1)}, bf16[688,4096]{1,0:T(8,128)(2,1)}, bf16[32,128]{1,0:T(8,128)(2,1)}) custom-call(bf16[688,4096]{1,0:T(8,128)(2,1)S(1)} %get-tuple-element.12.refs_0_, bf16[688,4096]{1,0:T(8,128)(2,1)S(1)} %get-tuple-element.13.refs_1_, bf16[688,4096]{1,0:T(8,128)(2,1)S(1)} %get-tuple-element.14.refs_2_, ...), custom_call_target="tpu_custom_call" | custom-call | tf_op jit(solution)/shard_map/pallas_call | solution.py:305
